TPU v7x, 32 devices: a whole 2x2x4 slice. The times are simulated.
32 devices in a mesh: groups: 2 (over x), tok: 16 (over z, y, core).
Axes of the slice: x: 2, y: 2, z: 4, core: 2. Of those that a mesh axis runs over, the one named last changes fastest.
Arguments:
- activations: bfloat16 [32, 128, 768], P(('groups', 'tok')), parts along dimension 0, may hold values from -32 to 32
- pair_repr: bfloat16 [256, 128, 128], P('groups', 'tok'), parts along dimension 0, may hold values from -6 to 6
- pair_gain: float32 [128], replicated, may hold values from 0.5 to 1.5
- bias_weight: float32 [128, 16], replicated, may hold values from -0.5 to 0.5
- proj_weight: bfloat16 [768, 3072], replicated, may hold values from -0.21875 to 0.21875
- query_bias: float32 [768], replicated, may hold values from -5 to 5
- out_weight: bfloat16 [768, 768], replicated, may hold values from -0.21875 to 0.21875
- token_mask: int32 [256], P('groups'), parts along dimension 0, may hold values 0 or 1
- out_cotangent: bfloat16 [32, 128, 768], P(('groups', 'tok')), parts along dimension 0, may hold values from -6 to 6
Outputs:
- grad_activations: bfloat16 [32, 128, 768], P(('groups', 'tok')), parts along dimension 0
- grad_pair: bfloat16 [256, 128, 128], P('groups', 'tok'), parts along dimension 0
- grad_proj: float32 [1536, 3072], P(('groups', 'tok')), parts along dimension 0
- grad_out_weight: float32 [1536, 768], P(('groups', 'tok')), parts along dimension 0
- grad_query_bias: float32 [1536], P('groups'), parts along dimension 0
- grad_bias_weight: float32 [256, 16], P('groups'), parts along dimension 0
- grad_pair_gain: float32 [256], P('groups'), parts along dimension 0
There are 2 independent parts, one for each index of `groups`. A program takes and returns all parts, laid end to end along the dimension named above; an argument that names none is the same for every part. Nothing has to cross between parts.
All inputs are finite; a program needn't handle non-finite values.
Results may differ from a plain program's by a relative error of at most 0.015.
The roundings to bfloat16 on the way count: a program that leaves them out, or rounds other values in their place, can miss the bound.
Values may be sent and summed in bfloat16 or wider, within the bound.
A program may use at most 128 MiB of HBM per device.

v0:
```python
import math
import jax
import jax.numpy as jnp
from jax import lax
from jax.sharding import PartitionSpec as P

HEADS = 16
HD = 48
EPSILON = 1e-05
MASK_PENALTY = 10000.0


def as_sent(value):
    return jax.tree.map(lambda a: a.astype(jnp.bfloat16) if a.dtype == jnp.float32 else a, value)


def partner(block, axis, apart):
    count = lax.axis_size(axis)
    route = []
    for low in range(count):
        high = low | 1 << apart
        if high != low and high < count:
            route += [(low, high), (high, low)]
    return lax.ppermute(block, axis, route)


def dest_order(tensor):
    return tensor.reshape((tensor.shape[0] * tensor.shape[1],) + tensor.shape[2:])


def source_heads(tensor, blocks):
    rest = tensor.shape[1:]
    return tensor.reshape((HEADS, blocks) + rest)


def row_blocks(tensor, blocks):
    channels = tensor.shape[0]
    block_rows = tensor.shape[3] // blocks
    shaped = tensor.reshape(channels, HEADS, HD, blocks, block_rows)
    return dest_order(shaped.transpose(1, 3, 0, 2, 4))


def token_rows(tensor, blocks):
    shaped = source_heads(tensor, blocks)
    channels = shaped.shape[2]
    block_rows = shaped.shape[4]
    return shaped.transpose(1, 4, 2, 0, 3).reshape(blocks * block_rows, channels * HEADS * HD)


def grouped(tree, group_size):
    return tree.reshape((tree.shape[0] // group_size, group_size) + tree.shape[1:])


def ungrouped(tree):
    return tree.reshape((tree.shape[0] * tree.shape[1],) + tree.shape[2:])


def xor_order(array, position, bit_count):
    for level in range(bit_count):
        shaped = array.reshape((array.shape[0] // (2 << level), 2, 1 << level) + array.shape[1:])
        bit_set = position // (1 << level) % 2
        array = jnp.where(bit_set == 1, shaped[:, ::-1], shaped).reshape(array.shape)
    return array


def group_regroup(array, position, bit_count, offset):
    holding = xor_order(array, position, bit_count)
    for level in range(bit_count):
        shaped = holding.reshape(
            (holding.shape[0] // (2 << level), 2, 1 << level) + holding.shape[1:]
        )
        arrived_half = partner(as_sent(shaped[:, 1]), "tok", offset + level)
        holding = jnp.stack([shaped[:, 0], arrived_half], axis=1).reshape(holding.shape)
    return xor_order(holding, position, bit_count)


def probabilities(query, keys, bias_full, key_bias):
    scores = jnp.einsum("di,dj->ij", query, keys, preferred_element_type=jnp.float32) * HD ** (-0.5)
    scores = scores + bias_full + key_bias[None, :]
    peak = jnp.max(scores, axis=1, keepdims=True)
    expo = jnp.exp(scores - peak)
    return expo / jnp.sum(expo, axis=1, keepdims=True)


def attend_forward(values, probs):
    return jnp.einsum(
        "dj,ij->di", values, probs.astype(jnp.bfloat16), preferred_element_type=jnp.float32
    ).astype(jnp.bfloat16)


def gate_terms(grad_gated, gate, attended):
    gate32 = gate.astype(jnp.float32)
    grad32 = grad_gated.astype(jnp.float32)
    att32 = attended.astype(jnp.float32)
    gated = (gate32 * att32).astype(jnp.bfloat16)
    grad_att = (grad32 * gate32).astype(jnp.bfloat16)
    grad_logit = (grad32 * att32 * gate32 * (1.0 - gate32)).astype(jnp.bfloat16)
    return (grad_att, grad_logit, gated)


def attend_back(query, keys, values, probs, grad_att):
    rounded = probs.astype(jnp.bfloat16)
    grad_value = jnp.einsum("di,ij->dj", grad_att, rounded, preferred_element_type=jnp.float32)
    grad_probs = jnp.einsum("di,dj->ij", grad_att, values, preferred_element_type=jnp.float32)
    grad_scores = probs * (grad_probs - jnp.sum(probs * grad_probs, axis=1, keepdims=True))
    scores_b = grad_scores.astype(jnp.bfloat16)
    grad_query = jnp.einsum(
        "ij,dj->di", scores_b, keys, preferred_element_type=jnp.float32
    ) * HD ** (-0.5)
    grad_key = jnp.einsum(
        "ij,di->dj", scores_b, query, preferred_element_type=jnp.float32
    ) * HD ** (-0.5)
    return (grad_query.astype(jnp.bfloat16), jnp.stack([grad_key, grad_value], axis=0), grad_scores)


def make_joint(bias_full, key_bias):

    def joint_one(front, kv_one):
        probs = probabilities(front[0], kv_one[0], bias_full, key_bias)
        attended_one = attend_forward(kv_one[1], probs)
        grad_att, grad_logit, gated_one = gate_terms(front[2], front[1], attended_one)
        grad_query, grad_kv, grad_scores = attend_back(
            front[0], kv_one[0], kv_one[1], probs, grad_att
        )
        return (jnp.stack([grad_query, grad_logit, gated_one], axis=0), grad_kv, grad_scores)

    return joint_one


def on_device(
    activations,
    pair_repr,
    pair_gain,
    bias_weight,
    proj_weight,
    query_bias,
    out_weight,
    token_mask,
    out_cotangent,
):
    tok_count = lax.axis_size("tok")
    blocks = tok_count // HEADS
    all_tokens = activations.shape[1]
    feature = activations.shape[2]
    block_rows = all_tokens // blocks
    bit_count = blocks.bit_length() - 1
    position = lax.axis_index("tok") % blocks
    offset = 0
    act_rows = activations.reshape(all_tokens, feature)
    cot_rows = out_cotangent.reshape(all_tokens, feature)
    proj = jnp.dot(act_rows, proj_weight, preferred_element_type=jnp.float32)
    shift = jnp.concatenate([query_bias, jnp.zeros((2 * feature,), jnp.float32)])
    qkv_rows = (proj[:, : 3 * feature] + shift[None, :]).astype(jnp.bfloat16)
    gate = jax.nn.sigmoid(proj[:, 3 * feature :]).astype(jnp.bfloat16)
    grad_gated = jnp.einsum(
        "rn,mn->rm", cot_rows, out_weight, preferred_element_type=jnp.float32
    ).astype(jnp.bfloat16)
    pair_f = pair_repr.astype(jnp.float32)
    mean_z = jnp.mean(pair_f, axis=-1, keepdims=True)
    centred = pair_f - mean_z
    rstd = lax.rsqrt(jnp.mean(centred * centred, axis=-1, keepdims=True) + EPSILON)
    normed = centred * rstd
    scaled = normed * pair_gain
    bias_cols = jnp.einsum(
        "ijc,ch->hij", scaled, bias_weight, precision=lax.Precision.HIGHEST
    ).astype(jnp.bfloat16)
    key_bias = (token_mask.astype(jnp.float32) - 1.0) * MASK_PENALTY
    joint_rows = jnp.concatenate([qkv_rows[:, :feature], gate, grad_gated], axis=1)
    bias_wide = jnp.broadcast_to(bias_cols[:, None], (HEADS, blocks) + bias_cols.shape[1:])
    bias_full = lax.all_to_all(
        dest_order(bias_wide), "tok", split_axis=0, concat_axis=2, tiled=True
    )[0].astype(jnp.float32)
    per_item = make_joint(bias_full, key_bias)
    five_rows = jnp.concatenate([joint_rows, qkv_rows[:, feature:]], axis=1)
    five_view = five_rows.reshape(all_tokens, 5, HEADS, HD).transpose(1, 2, 3, 0)
    arrived = lax.all_to_all(
        row_blocks(five_view, blocks), "tok", split_axis=0, concat_axis=0, tiled=True
    )
    regrouped = group_regroup(
        arrived.reshape((blocks, HEADS) + arrived.shape[1:]), position, bit_count, offset
    )
    head_items = regrouped.transpose(1, 2, 3, 0, 4).reshape(HEADS, 5, HD, all_tokens)
    group_size = math.gcd(HEADS, max(1, 512 // all_tokens))

    def sample_step(total, pieces):
        merged, grad_kv, grad_scores = jax.vmap(per_item)(pieces[:, :3], pieces[:, 3:])
        results = jnp.concatenate([merged, grad_kv.astype(jnp.bfloat16)], axis=1)
        return (total + jnp.sum(grad_scores, axis=0), results)

    start_total = jnp.zeros((all_tokens, all_tokens), jnp.float32)
    grad_bias_part, results = lax.scan(sample_step, start_total, grouped(head_items, group_size))
    results = ungrouped(results)
    outgoing = results.reshape(HEADS, 5, HD, blocks, block_rows).transpose(3, 0, 1, 2, 4)
    returned = group_regroup(outgoing, position, bit_count, offset).reshape(
        tok_count, 5, HD, block_rows
    )
    came_back = lax.all_to_all(returned, "tok", split_axis=0, concat_axis=0, tiled=True)
    rows_back = token_rows(came_back, blocks)
    grad_rows = jnp.concatenate(
        [rows_back[:, :feature], rows_back[:, 3 * feature :], rows_back[:, feature : 2 * feature]],
        axis=1,
    )
    gated = rows_back[:, 2 * feature : 3 * feature]
    received = lax.all_to_all(
        grad_bias_part[None].astype(jnp.bfloat16), "tok", split_axis=2, concat_axis=0, tiled=True
    ).astype(jnp.float32)
    grad_bias = jnp.sum(source_heads(received, blocks), axis=1)
    first = jnp.einsum("rc,rn->cn", act_rows, grad_rows, preferred_element_type=jnp.float32)
    second = jnp.einsum("rc,rn->cn", gated, cot_rows, preferred_element_type=jnp.float32)
    weight_grads = lax.psum_scatter(
        jnp.concatenate([first, second], axis=1), "tok", scatter_dimension=0, tiled=True
    )
    grad_activations = jnp.einsum(
        "rn,dn->rd", grad_rows, proj_weight, preferred_element_type=jnp.float32
    ).astype(jnp.bfloat16)
    grad_zg = jnp.einsum("hij,ch->ijc", grad_bias, bias_weight, precision=lax.Precision.HIGHEST)
    weight_part = jnp.einsum("ijc,hij->ch", scaled, grad_bias, precision=lax.Precision.HIGHEST)
    gain_part = jnp.sum(normed * grad_zg, axis=(0, 1))
    query_part = jnp.sum(grad_rows[:, :feature].astype(jnp.float32), axis=0)
    grad_query_bias, grad_bias_weight, grad_pair_gain = lax.psum(
        (query_part, weight_part, gain_part), "tok"
    )
    grad_norm = grad_zg * pair_gain
    grad_pair = (
        grad_norm
        - jnp.mean(grad_norm, axis=-1, keepdims=True)
        - normed * jnp.mean(grad_norm * normed, axis=-1, keepdims=True)
    ) * rstd
    return (
        grad_activations.reshape(1, all_tokens, feature),
        grad_pair.astype(jnp.bfloat16),
        weight_grads[:, : 4 * feature],
        weight_grads[:, 4 * feature :],
        grad_query_bias,
        grad_bias_weight,
        grad_pair_gain,
    )


def solution(mesh):
    in_specs = (
        P(("groups", "tok"), None, None),
        P("groups", "tok", None),
        P(),
        P(),
        P(),
        P(),
        P(),
        P("groups"),
        P(("groups", "tok"), None, None),
    )
    out_specs = (
        P(("groups", "tok"), None, None),
        P("groups", "tok", None),
        P(("groups", "tok"), None),
        P(("groups", "tok"), None),
        P("groups"),
        P("groups", None),
        P("groups"),
    )
    return jax.shard_map(
        on_device, mesh=mesh, in_specs=in_specs, out_specs=out_specs, check_vma=False
    )
```

profile of v0, /device:TPU:0, one launch (start us, length us, event | category | flops | bytes accessed | tf_op | source)
XLA Modules:
  0.0 252.7 jit_solution(9659718730812204163)
XLA Ops:
  7.2 1.2 copy.67
  8.6 1.2 fusion.28
  10.4 7.4 %all-to-all-start.1 = ((bf16[16,128,8]{1,2,0:T(8,128)(2,1)}), bf16[16,128,8]{1,2,0:T(8,128)(2,1)S(1)}, u32[]{:S(2)}, u32[]{:S(2)}) async-start(bf16[16,128,8]{1,2,0:T(8,128)(2,1)} %copy.69), calls=%async_computation.1 | async-start | bytes 65536 | tf_op jit(solution)/shard_map/all_to_all | solution.py:170
  17.9 3.2 %fusion.58 = f32[128,3072]{1,0:T(8,128)S(1)} fusion(bf16[768,3072]{1,0:T(8,128)(2,1)} %param.15, bf16[1,128,768]{2,1,0:T(8,128)(2,1)} %param.11), kind=kOutput, calls=%fused_computation.93 | convolution fusion | flops 603979776 | bytes 6488064 | tf_op jit(solution)/shard_map/dot_general | solution.py:151
  23.3 1.0 copy.66
  24.5 5.9 %all-to-all-start = ((bf16[16,5,48,128]{3,2,1,0:T(8,128)(2,1)}), bf16[16,5,48,128]{3,2,1,0:T(8,128)(2,1)S(1)}, u32[]{:S(2)}, u32[]{:S(2)}) async-start(bf16[16,5,48,128]{3,2,1,0:T(8,128)(2,1)} %copy.66), calls=%async_computation | async-start | bytes 1966080 | tf_op jit(solution)/shard_map/all_to_all | solution.py:176
  30.5 21.7 %all-to-all-done = bf16[16,5,48,128]{3,2,1,0:T(8,128)(2,1)S(1)} async-done(((bf16[16,5,48,128]{3,2,1,0:T(8,128)(2,1)}), bf16[16,5,48,128]{3,2,1,0:T(8,128)(2,1)S(1)}, u32[]{:S(2)}, u32[]{:S(2)}) %all-to-all-start) | async-done | bytes 983072 | tf_op jit(solution)/shard_map/all_to_all | solution.py:176
  52.2 10.9 %while.13 = (s32[]{:T(128)}, f32[128,128]{0,1:T(8,128)S(1)}, bf16[4,4,5,48,128]{4,3,2,1,0:T(8,128)(2,1)}, bf16[4,4,5,48,128]{4,3,2,1,0:T(8,128)(2,1)S(1)}, f32[1...) while((s32[]{:T(128)}, f32[128,128]{0,1:T(8,128)S(1)}, ...), condition=%wide.region_7.8_spmd.clone, body=%wide.region_2.7_spmd.clone.sunk | while | flops 52896640 | bytes 4685423 | solution.py:191
  59.7 0.7 copy_dynamic-update-slice_fusion.2
  62.4 0.7 copy_dynamic-update-slice_fusion.2
  63.1 30.0 %all_to_all.34 = bf16[16,5,48,128]{3,2,1,0:T(8,128)(2,1)S(1)} all-to-all(bf16[16,5,48,128]{3,2,1,0:T(8,128)(2,1)} %bitcast.220), channel_id=1, replica_groups=mesh['groups'=2,'tok'=16] {'tok'}, dimensions={0} | all-to-all | bytes 1966080 | tf_op jit(solution)/shard_map/all_to_all | solution.py:197
  93.3 0.8 copy-done.2
  94.6 1.4 convolution_bitcast_fusion
  95.9 4.6 %pad_maximum_fusion = f32[768,3840]{0,1:T(8,128)} fusion(f32[768,768]{0,1:T(8,128)S(1)} %fusion.53, f32[768,3072]{0,1:T(8,128)S(1)} %convolution_bitcast_fusion), kind=kLoop, calls=%fused_computation.49 | loop fusion | flops 2949120 | bytes 23592960 | tf_op jit(solution)/shard_map/concatenate | solution.py:211
  100.6 12.4 %copy.86 = f32[768,3840]{1,0:T(8,128)} copy(f32[768,3840]{0,1:T(8,128)} %pad_maximum_fusion) | data formatting | bytes 23592960
  113.8 0.8 reduce
  114.6 11.2 %all_to_all.35 = bf16[16,2,512]{2,1,0:T(2,128)(2,1)S(1)} all-to-all(bf16[16,2,512]{2,1,0:T(2,128)(2,1)S(1)} %reshape.98), channel_id=1, replica_groups=mesh['groups'=2,'tok'=16] {'tok'}, dimensions={0} | all-to-all | bytes 65536 | tf_op jit(solution)/shard_map/all_to_all | solution.py:204
  126.7 0.9 copy.77
  127.6 1.2 convolution_bitcast_fusion.1
  129.0 60.7 %all-reduce.1 = (f32[768]{0:T(1024)}, f32[128,16]{0,1:T(8,128)}, f32[128]{0:T(128)}) all-reduce(f32[768]{0:T(1024)S(1)} %convert_reduce_fusion.1, f32[128,16]{0,1:T(8,128)S(1)} %convolution_bitcast_fusion.1, f32[128]{0:T(128)S(1)} %get-tuple-element.109), channel_id=1, replica_groups=mesh['groups'=2,'tok'=16] {'tok'}, use_global_device_ids=true, to_apply=%region_12.13 | all-reduce | flops 2944 | bytes 23552 | tf_op jit(solution)/shard_map/psum | solution.py:220
  189.7 4.7 %fusion.27 = bf16[1,128,768]{2,1,0:T(8,128)(2,1)} fusion(bf16[768,3072]{1,0:T(8,128)(2,1)} %param.15, bf16[128,768]{0,1:T(8,128)(2,1)S(1)} %get-tuple-element.136, bf16[128,1536]{0,1:T(8,128)(2,1)S(1)} %slice.80, bf16[128,768]{0,1:T(8,128)(2,1)S(1)} %get-tuple-element.135), kind=kOutput, calls=%fused_computation.55 | convolution fusion | flops 606437376 | bytes 5701632 | tf_op jit(solution)/shard_map/rn,dn->rd/dot_general | solution.py:213
  194.4 48.0 %reduce-scatter.4.cloned.1.call-done = f32[48,3840]{1,0:T(8,128)} async-done(((f32[768,3840]{1,0:T(8,128)}), f32[48,3840]{1,0:T(8,128)}) %reduce-scatter.4.cloned.1.call-update) | async-done | bytes 737296
  242.4 1.6 slice.84
  244.0 1.9 slice.83
  (97 shorter events, 14.7 us)
Async XLA Ops:
  7.2 14.2 %copy-start = (bf16[768,768]{1,0:T(8,128)(2,1)S(1)}, bf16[768,768]{1,0:T(8,128)(2,1)}, u32[]{:S(2)}) copy-start(bf16[768,768]{1,0:T(8,128)(2,1)} %param.17) | copy-start | bytes 3538948
  10.4 14.1 %all-to-all-start.1 = ((bf16[16,128,8]{1,2,0:T(8,128)(2,1)}), bf16[16,128,8]{1,2,0:T(8,128)(2,1)S(1)}, u32[]{:S(2)}, u32[]{:S(2)}) async-start(bf16[16,128,8]{1,2,0:T(8,128)(2,1)} %copy.69), calls=%async_computation.1 | async-start | bytes 65536 | tf_op jit(solution)/shard_map/all_to_all | solution.py:170
  17.8 3.4 %copy-start.5 = (f32[768]{0:T(1024)S(1)}, f32[768]{0:T(1024)}, u32[]{:S(2)}) copy-start(f32[768]{0:T(1024)} %param.16) | copy-start | bytes 9220
  21.1 0.9 copy-start.1
  23.3 7.2 %copy-start.8 = (s32[128]{0:T(128)S(1)}, s32[128]{0:T(128)}, u32[]{:S(2)}) copy-start(s32[128]{0:T(128)} %param.18) | copy-start | bytes 1540
  24.5 27.8 %all-to-all-start = ((bf16[16,5,48,128]{3,2,1,0:T(8,128)(2,1)}), bf16[16,5,48,128]{3,2,1,0:T(8,128)(2,1)S(1)}, u32[]{:S(2)}, u32[]{:S(2)}) async-start(bf16[16,5,48,128]{3,2,1,0:T(8,128)(2,1)} %copy.66), calls=%async_computation | async-start | bytes 1966080 | tf_op jit(solution)/shard_map/all_to_all | solution.py:176
  30.4 212.0 %reduce-scatter.4.cloned.1.call-start = ((), (), s32[]{:S(2)}) async-start(), calls=%async_computation.5 | async-start | bytes 12533760
  93.1 0.9 copy-start.2
  93.2 1.3 copy-start.3
  113.0 12.9 %copy-start.6 = (f32[128]{0:T(128)S(1)}, f32[128]{0:T(128)}, u32[]{:S(2)}) copy-start(f32[128]{0:T(128)} %param.13) | copy-start | bytes 1540
  113.0 12.9 %copy-start.7 = (f32[128,16]{0,1:T(8,128)S(1)}, f32[128,16]{0,1:T(8,128)}, u32[]{:S(2)}) copy-start(f32[128,16]{0,1:T(8,128)} %param.14) | copy-start | bytes 24580
  125.9 0.7 copy-start.4
Sparse Core Ops, SparseCore 0:
  113.2 129.1 reduce-scatter.3
where the time goes:
time: 254 us; the launch traced here: 253 us
  blocking collectives  102 us (40%)
  waiting for transfers between devices  69.8 us (27%)
  local copies, waits for them, and re-layouts  22.9 us (9%)
  matrix products  20.6 us (8%)
  between operations  14.4 us (6%)
  starting transfers between devices  13.4 us (5%)
  other arithmetic  9.52 us (4%)
    psum x1, blocking collectives, on_device(): lax.psum((query_part, weight_part, gain_part), 'tok')  60.7 us
    unnamed x2, waiting for transfers between devices  48 us
    all_to_all x1, blocking collectives, on_device(): lax.all_to_all(returned, 'tok', split_axis=0, concat_axis=0, tiled=True)  30 us
    all_to_all x1, waiting for transfers between devices, on_device(): lax.all_to_all(row_blocks(five_view, blocks), 'tok', split_axis=0, concat...  21.7 us
    unnamed x25, local copies, waits for them, and re-layouts  16.6 us
    all_to_all x1, blocking collectives, on_device(): lax.all_to_all(grad_bias_part[None].astype(jnp.bfloat16), 'tok', split_ax...  11.2 us
    all_to_all x1, starting transfers between devices, on_device(): lax.all_to_all(dest_order(bias_wide), 'tok', split_axis=0, concat_axis=2,...  7.41 us
    all_to_all x1, starting transfers between devices, on_device(): lax.all_to_all(row_blocks(five_view, blocks), 'tok', split_axis=0, concat...  5.91 us
  transfers between devices with their start and end apart: 3, of which 3 were waited for; matrix products, arithmetic and copies ran while one was open for 6% of the time, Pallas kernels for 0%

commit v1 on v0

--- a/solution.py
+++ b/solution.py
@@ -3,6 +3,7 @@
 import jax.numpy as jnp
 from jax import lax
 from jax.sharding import PartitionSpec as P
+from jax.lax import all_to_all, axis_size
 
 HEADS = 16
 HD = 48
@@ -167,9 +168,15 @@
     key_bias = (token_mask.astype(jnp.float32) - 1.0) * MASK_PENALTY
     joint_rows = jnp.concatenate([qkv_rows[:, :feature], gate, grad_gated], axis=1)
     bias_wide = jnp.broadcast_to(bias_cols[:, None], (HEADS, blocks) + bias_cols.shape[1:])
-    bias_full = lax.all_to_all(
-        dest_order(bias_wide), "tok", split_axis=0, concat_axis=2, tiled=True
-    )[0].astype(jnp.float32)
+
+    def change_stacks_all_up(load, which_dim, axis_k):
+        heard = axis_size("tok")
+        n_now = jnp.split(load, heard, axis=which_dim)
+        y_new = jnp.stack(n_now)
+        vec_out = all_to_all(y_new, concat_axis=0, split_axis=0, axis_name="tok")
+        return jnp.concatenate(vec_out, axis=axis_k)
+
+    bias_full = change_stacks_all_up(dest_order(bias_wide), 0, 2)[0].astype(jnp.float32)
     per_item = make_joint(bias_full, key_bias)
     five_rows = jnp.concatenate([joint_rows, qkv_rows[:, feature:]], axis=1)
     five_view = five_rows.reshape(all_tokens, 5, HEADS, HD).transpose(1, 2, 3, 0)

time: 254 us -> 262 us (1.031)
  local copies, waits for them, and re-layouts: 22.9 us -> 31.6 us
    unnamed x25 -> x42, local copies, waits for them, and re-layouts: 16.6 us -> 25.3 us
where the time goes in v1:
time: 262 us; the launch traced here: 261 us
  blocking collectives  102 us (39%)
  waiting for transfers between devices  69.9 us (27%)
  local copies, waits for them, and re-layouts  31.6 us (12%)
  matrix products  20.5 us (8%)
  between operations  14.4 us (5%)
  starting transfers between devices  13.3 us (5%)
  other arithmetic  9.52 us (4%)
    psum x1, blocking collectives, on_device(): lax.psum((query_part, weight_part, gain_part), 'tok')  60.7 us
    unnamed x2, waiting for transfers between devices  48 us
    all_to_all x1, blocking collectives, on_device(): lax.all_to_all(returned, 'tok', split_axis=0, concat_axis=0, tiled=True)  30 us
    unnamed x42, local copies, waits for them, and re-layouts  25.3 us
    all_to_all x1, waiting for transfers between devices, on_device(): lax.all_to_all(row_blocks(five_view, blocks), 'tok', split_axis=0, concat...  21.7 us
    all_to_all x1, blocking collectives, on_device(): lax.all_to_all(grad_bias_part[None].astype(jnp.bfloat16), 'tok', split_ax...  11.2 us
    all_to_all x1, starting transfers between devices, change_stacks_all_up(): vec_out = all_to_all(y_new, concat_axis=0, split_axis=0, axis_name='tok')  7.41 us
    all_to_all x1, starting transfers between devices, on_device(): lax.all_to_all(row_blocks(five_view, blocks), 'tok', split_axis=0, concat...  5.8 us
  transfers between devices with their start and end apart: 3, of which 3 were waited for; matrix products, arithmetic and copies ran while one was open for 6% of the time, Pallas kernels for 0%

profile of v1, /device:TPU:0, one launch (start us, length us, event | category | flops | bytes accessed | tf_op | source)
XLA Modules:
  0.0 261.4 jit_solution(17716955801403759428)
XLA Ops:
  7.2 1.3 copy.440
  8.6 1.2 fusion.28
  19.2 7.4 %all-to-all-start.1 = ((bf16[16,1,128,8]{2,3,1,0:T(8,128)(2,1)}), bf16[16,1,128,8]{2,3,1,0:T(8,128)(2,1)S(1)}, u32[]{:S(2)}, u32[]{:S(2)}) async-start(bf16[16,1,128,8]{2,3,1,0:T(8,128)(2,1)} %constant_dynamic-update-slice_fusion), calls=%async_computation.1 | async-start | bytes 65536 | tf_op jit(solution)/shard_map/all_to_all | solution.py:176
  26.6 3.1 %fusion.58 = f32[128,3072]{1,0:T(8,128)S(1)} fusion(bf16[768,3072]{1,0:T(8,128)(2,1)} %param.15, bf16[1,128,768]{2,1,0:T(8,128)(2,1)S(1)} %copy-done.3), kind=kOutput, calls=%fused_computation.93 | convolution fusion | flops 603979776 | bytes 6488064 | tf_op jit(solution)/shard_map/dot_general | solution.py:152
  32.0 1.0 copy.439
  33.2 5.8 %all-to-all-start = ((bf16[16,5,48,128]{3,2,1,0:T(8,128)(2,1)}), bf16[16,5,48,128]{3,2,1,0:T(8,128)(2,1)S(1)}, u32[]{:S(2)}, u32[]{:S(2)}) async-start(bf16[16,5,48,128]{3,2,1,0:T(8,128)(2,1)} %copy.439), calls=%async_computation | async-start | bytes 1966080 | tf_op jit(solution)/shard_map/all_to_all | solution.py:183
  39.1 21.7 %all-to-all-done = bf16[16,5,48,128]{3,2,1,0:T(8,128)(2,1)S(1)} async-done(((bf16[16,5,48,128]{3,2,1,0:T(8,128)(2,1)}), bf16[16,5,48,128]{3,2,1,0:T(8,128)(2,1)S(1)}, u32[]{:S(2)}, u32[]{:S(2)}) %all-to-all-start) | async-done | bytes 983072 | tf_op jit(solution)/shard_map/all_to_all | solution.py:183
  60.9 10.9 %while.13 = (s32[]{:T(128)}, f32[128,128]{0,1:T(8,128)S(1)}, bf16[4,4,5,48,128]{4,3,2,1,0:T(8,128)(2,1)}, bf16[4,4,5,48,128]{4,3,2,1,0:T(8,128)(2,1)S(1)}, f32[1...) while((s32[]{:T(128)}, f32[128,128]{0,1:T(8,128)S(1)}, ...), condition=%wide.region_7.8_spmd.clone, body=%wide.region_2.7_spmd.clone.sunk | while | flops 52896640 | bytes 4685423 | solution.py:198
  68.3 0.7 copy_dynamic-update-slice_fusion.2
  71.1 0.7 copy_dynamic-update-slice_fusion.2
  71.8 30.0 %all_to_all.30 = bf16[16,5,48,128]{3,2,1,0:T(8,128)(2,1)S(1)} all-to-all(bf16[16,5,48,128]{3,2,1,0:T(8,128)(2,1)} %bitcast.249), channel_id=1, replica_groups=mesh['groups'=2,'tok'=16] {'tok'}, dimensions={0} | all-to-all | bytes 1966080 | tf_op jit(solution)/shard_map/all_to_all | solution.py:204
  101.9 0.8 copy-done.2
  103.2 1.4 convolution_bitcast_fusion
  104.6 4.6 %pad_maximum_fusion = f32[768,3840]{0,1:T(8,128)} fusion(f32[768,768]{0,1:T(8,128)S(1)} %fusion.53, f32[768,3072]{0,1:T(8,128)S(1)} %convolution_bitcast_fusion), kind=kLoop, calls=%fused_computation.49 | loop fusion | flops 2949120 | bytes 23592960 | tf_op jit(solution)/shard_map/concatenate | solution.py:218
  109.2 12.4 %copy.458 = f32[768,3840]{1,0:T(8,128)} copy(f32[768,3840]{0,1:T(8,128)} %pad_maximum_fusion) | data formatting | bytes 23592960
  122.4 0.8 reduce
  123.3 11.2 %all_to_all.31 = bf16[16,2,512]{2,1,0:T(2,128)(2,1)S(1)} all-to-all(bf16[16,2,512]{2,1,0:T(2,128)(2,1)S(1)} %reshape.95), channel_id=1, replica_groups=mesh['groups'=2,'tok'=16] {'tok'}, dimensions={0} | all-to-all | bytes 65536 | tf_op jit(solution)/shard_map/all_to_all | solution.py:211
  135.4 0.9 copy.449
  136.3 1.2 convolution_bitcast_fusion.1
  137.6 60.7 %all-reduce.1 = (f32[768]{0:T(1024)}, f32[128,16]{0,1:T(8,128)}, f32[128]{0:T(128)}) all-reduce(f32[768]{0:T(1024)S(1)} %convert_reduce_fusion.1, f32[128,16]{0,1:T(8,128)S(1)} %convolution_bitcast_fusion.1, f32[128]{0:T(128)S(1)} %get-tuple-element.304), channel_id=1, replica_groups=mesh['groups'=2,'tok'=16] {'tok'}, use_global_device_ids=true, to_apply=%region_12.13 | all-reduce | flops 2944 | bytes 23552 | tf_op jit(solution)/shard_map/psum | solution.py:227
  198.3 4.7 %fusion.27 = bf16[1,128,768]{2,1,0:T(8,128)(2,1)} fusion(bf16[768,3072]{1,0:T(8,128)(2,1)} %param.15, bf16[128,768]{0,1:T(8,128)(2,1)S(1)} %get-tuple-element.331, bf16[128,1536]{0,1:T(8,128)(2,1)S(1)} %slice.80, bf16[128,768]{0,1:T(8,128)(2,1)S(1)} %get-tuple-element.330), kind=kOutput, calls=%fused_computation.55 | convolution fusion | flops 606437376 | bytes 5701632 | tf_op jit(solution)/shard_map/rn,dn->rd/dot_general | solution.py:220
  203.0 48.0 %reduce-scatter.4.cloned.1.call-done = f32[48,3840]{1,0:T(8,128)} async-done(((f32[768,3840]{1,0:T(8,128)}), f32[48,3840]{1,0:T(8,128)}) %reduce-scatter.4.cloned.1.call-update) | async-done | bytes 737296
  251.0 1.6 slice.84
  252.6 1.9 slice.83
  (115 shorter events, 23.5 us)
Async XLA Ops:
  7.2 22.9 %copy-start = (bf16[768,768]{1,0:T(8,128)(2,1)S(1)}, bf16[768,768]{1,0:T(8,128)(2,1)}, u32[]{:S(2)}) copy-start(bf16[768,768]{1,0:T(8,128)(2,1)} %param.17) | copy-start | bytes 3538948
  7.2 19.4 %copy-start.3 = (bf16[1,128,768]{2,1,0:T(8,128)(2,1)S(1)}, bf16[1,128,768]{2,1,0:T(8,128)(2,1)}, u32[]{:S(2)}) copy-start(bf16[1,128,768]{2,1,0:T(8,128)(2,1)} %param.11) | copy-start | bytes 589828
  19.2 14.1 %all-to-all-start.1 = ((bf16[16,1,128,8]{2,3,1,0:T(8,128)(2,1)}), bf16[16,1,128,8]{2,3,1,0:T(8,128)(2,1)S(1)}, u32[]{:S(2)}, u32[]{:S(2)}) async-start(bf16[16,1,128,8]{2,3,1,0:T(8,128)(2,1)} %constant_dynamic-update-slice_fusion), calls=%async_computation.1 | async-start | bytes 65536 | tf_op jit(solution)/shard_map/all_to_all | solution.py:176
  26.6 3.3 %copy-start.6 = (f32[768]{0:T(1024)S(1)}, f32[768]{0:T(1024)}, u32[]{:S(2)}) copy-start(f32[768]{0:T(1024)} %param.16) | copy-start | bytes 9220
  29.7 0.9 copy-start.1
  32.0 7.2 %copy-start.9 = (s32[128]{0:T(128)S(1)}, s32[128]{0:T(128)}, u32[]{:S(2)}) copy-start(s32[128]{0:T(128)} %param.18) | copy-start | bytes 1540
  33.2 27.6 %all-to-all-start = ((bf16[16,5,48,128]{3,2,1,0:T(8,128)(2,1)}), bf16[16,5,48,128]{3,2,1,0:T(8,128)(2,1)S(1)}, u32[]{:S(2)}, u32[]{:S(2)}) async-start(bf16[16,5,48,128]{3,2,1,0:T(8,128)(2,1)} %copy.439), calls=%async_computation | async-start | bytes 1966080 | tf_op jit(solution)/shard_map/all_to_all | solution.py:183
  39.0 212.0 %reduce-scatter.4.cloned.1.call-start = ((), (), s32[]{:S(2)}) async-start(), calls=%async_computation.5 | async-start | bytes 12533760
  101.7 0.9 copy-start.2
  101.9 1.3 copy-start.4
  121.6 12.9 %copy-start.7 = (f32[128]{0:T(128)S(1)}, f32[128]{0:T(128)}, u32[]{:S(2)}) copy-start(f32[128]{0:T(128)} %param.13) | copy-start | bytes 1540
  121.6 12.9 %copy-start.8 = (f32[128,16]{0,1:T(8,128)S(1)}, f32[128,16]{0,1:T(8,128)}, u32[]{:S(2)}) copy-start(f32[128,16]{0,1:T(8,128)} %param.14) | copy-start | bytes 24580
  134.5 0.7 copy-start.5
Sparse Core Ops, SparseCore 0:
  121.8 129.1 reduce-scatter.3
